TPU v7x, 256 devices: a whole 4x4x8 slice. The times are simulated.
256 devices in a mesh: dp: 32 (over x, z_lo, core), head: 8 (over y, z_hi).
Axes of the slice: x: 4, y: 4, z: 8 (z_hi: 2, z_lo: 4; z = z_hi * 4 + z_lo), core: 2. Of those that a mesh axis runs over, the one named last changes fastest.
Arguments:
- frames_in: bfloat16 [32, 8, 320, 640], P('dp', 'head'), may hold values from -6 to 6
- ln1_gain: float32 [1280], replicated, may hold values from 0.25 to 1.75
- ln1_bias: float32 [1280], replicated, may hold values from -3 to 3
- qkv_weight: bfloat16 [1280, 3, 1024], P('dp', None, 'head'), may hold values from -0.1875 to 0.1875
- qv_bias: float32 [2, 1024], P(None, 'head'), may hold values from -3 to 3
- out_weight: bfloat16 [1024, 1280], P(('head', 'dp')), may hold values from -0.1875 to 0.1875
- out_bias: float32 [1280], P('head'), may hold values from -3 to 3
- ln2_gain: float32 [1280], replicated, may hold values from 0.25 to 1.75
- ln2_bias: float32 [1280], replicated, may hold values from -3 to 3
- fc1_weight: bfloat16 [1280, 5120], P('dp', 'head'), may hold values from -0.15625 to 0.15625
- fc1_bias: float32 [5120], P('head'), may hold values from -3 to 3
- fc2_weight: bfloat16 [5120, 1280], P(('head', 'dp')), may hold values from -0.078125 to 0.078125
- fc2_bias: float32 [1280], P('head'), may hold values from -3 to 3
- server_of_clip: int32 [32], replicated, may hold values from 0 to 7
Outputs:
- encoded: bfloat16 [32, 8, 320, 640], P('dp', 'head')
All inputs are finite; a program needn't handle non-finite values.
Results may differ from a plain program's by a relative error of at most 0.014.
Values may be sent and summed in bfloat16 or wider, within the bound.
No kernel may reach another device: no remote copies, remote signals or barrier semaphores. Data moves between devices by JAX's collectives and lax.ppermute only.
A program may use at most 64 MiB of HBM per device.

v0:
```python
import jax
import jax.numpy as jnp
from jax import lax
from jax.sharding import Mesh
from jax.sharding import PartitionSpec as P

HDIM = 64
DP = ("x", "zl", "core")
HEAD = ("y", "zh")
EPS = 1e-05


def exchange(value, axes):
    return lax.all_to_all(value, axes, split_axis=0, concat_axis=0, tiled=True)


def gather_y(value):
    copies = jnp.broadcast_to(value[None], (4, *value.shape))
    return exchange(copies, "y").reshape(4 * value.shape[0], value.shape[1])


def norm_columns(matrix, gain, shift):
    floats = matrix.astype(jnp.float32)
    center = jnp.mean(floats, axis=0, keepdims=True)
    spread = jnp.mean(jnp.square(floats - center), axis=0, keepdims=True)
    return ((floats - center) * lax.rsqrt(spread + EPS) * gain[:, None] + shift[:, None]).astype(
        jnp.bfloat16
    )


def dot_rows(left, right):
    return lax.dot_general(
        left, right, (((0,), (0,)), ((), ())), preferred_element_type=jnp.float32
    )


def slot_order(server_list):
    clip_count = server_list.shape[0]
    indices = jnp.arange(clip_count, dtype=jnp.int32)
    earlier = (server_list[None, :] < server_list[:, None]) | (
        server_list[None, :] == server_list[:, None]
    ) & (indices[None, :] < indices[:, None])
    slot_of = jnp.sum(earlier.astype(jnp.int32), axis=1)
    return jnp.sum(jnp.where(slot_of[None, :] == indices[:, None], indices[None, :], 0), axis=1)


def attend(queries, key_rows, value_rows):
    outs = []
    for at in range(0, queries.shape[0], HDIM):
        scores = dot_rows(key_rows[at : at + HDIM], queries[at : at + HDIM])
        maxima = jnp.max(scores, axis=0, keepdims=True)
        weights = jnp.exp(scores - maxima)
        probs = (weights / jnp.sum(weights, axis=0, keepdims=True)).astype(jnp.bfloat16)
        outs.append(
            jnp.dot(value_rows[at : at + HDIM], probs, preferred_element_type=jnp.float32).astype(
                jnp.bfloat16
            )
        )
    return jnp.concatenate(outs, axis=0)


def on_device(
    frames_in,
    ln1_gain,
    ln1_bias,
    qkv_weight,
    qv_bias,
    out_weight,
    out_bias,
    ln2_gain,
    ln2_bias,
    fc1_weight,
    fc1_bias,
    fc2_weight,
    fc2_bias,
    server_of_clip,
):
    bf16 = jnp.bfloat16
    y_at, core_at, zh_at = (lax.axis_index("y"), lax.axis_index("core"), lax.axis_index("zh"))
    plane = ("zh", "x", "zl", "core")
    w_qkv = lax.all_gather(qkv_weight.reshape(40, 384), plane, axis=0, tiled=True)
    w_out = lax.all_gather(out_weight, ("y",) + plane, axis=0, tiled=True)
    w_one = lax.all_gather(fc1_weight, plane, axis=0, tiled=True)
    w_two = lax.all_gather(fc2_weight, plane, axis=0, tiled=True)
    own = jnp.concatenate([qv_bias[0], qv_bias[1], fc1_bias, fc2_bias, out_bias])
    other = lax.ppermute(own, "zh", [(0, 1), (1, 0)])
    both = jnp.where(zh_at == 0, jnp.stack([own, other]), jnp.stack([other, own]))
    q_bias = both[:, 0:128].reshape(256, 1)
    v_bias = both[:, 128:256].reshape(256, 1)
    one_bias = both[:, 256:896].reshape(1280, 1)
    two_bias = both[:, 896:1056].reshape(320, 1)
    out_pair = both[:, 1056:1216].reshape(320)
    out_all = jnp.zeros((4, 320), jnp.float32)
    out_all = lax.dynamic_update_slice(out_all, out_pair[None], (y_at, 0))
    for step in (1, 2, 3):
        part = lax.ppermute(out_pair, "y", [(at, (at + step) % 4) for at in range(4)])
        out_all = lax.dynamic_update_slice(out_all, part[None], ((y_at - step) % 4, 0))
    out_all = out_all.reshape(1280, 1)
    clip_order = slot_order(server_of_clip)
    source_at = clip_order % 2 * 16 + clip_order // 2
    source_at = source_at.reshape(16, 2).T.reshape(32)
    pieces = frames_in[0, 0].reshape(2, 160, 4, 160).transpose(0, 3, 2, 1).reshape(32, 10, 640)
    shuffled = exchange(pieces, ("core", "x", "zl"))
    picked = jnp.take(shuffled, source_at, axis=0)
    block = exchange(picked, ("zh", "x", "zl")).reshape(320, 640)
    residual = gather_y(block)
    normed_one = norm_columns(residual, ln1_gain, ln1_bias)
    halves = [dot_rows(w_qkv[at : at + 1280], normed_one) for at in (0, 1280)]
    queries = jnp.concatenate([half[0:128] for half in halves], axis=0)
    queries = ((queries + q_bias) * HDIM ** (-0.5)).astype(bf16)
    keys = jnp.concatenate([half[128:256] for half in halves], axis=0).astype(bf16)
    values = jnp.concatenate([half[256:384] for half in halves], axis=0)
    values = (values + v_bias).astype(bf16)
    mine = jnp.concatenate([keys, values], axis=0)
    theirs = lax.ppermute(mine, "core", [(0, 1), (1, 0)])
    every = jnp.concatenate([mine, theirs], axis=1)
    context = attend(queries, every[:256], every[256:])
    whole_context = gather_y(context)
    attended = (residual.astype(jnp.float32) + out_all + dot_rows(w_out, whole_context)).astype(
        bf16
    )
    normed_two = norm_columns(attended, ln2_gain, ln2_bias)
    sums = jnp.concatenate(
        [dot_rows(w_one[at : at + 1280], normed_two) for at in (0, 1280)], axis=0
    )
    hidden = jax.nn.gelu(sums + one_bias, approximate=False).astype(bf16)
    terms = dot_rows(w_two, hidden).astype(bf16).reshape(4, 320, 640)
    arrived = exchange(terms, "y").astype(jnp.float32)
    kept = lax.dynamic_slice(attended, (y_at * 320, 0), (320, 640)).astype(jnp.float32)
    done = (kept + two_bias + jnp.sum(arrived, axis=0)).astype(bf16).reshape(2, 160, 640)
    same = [(j * 2 + k, k * 2 + j) for k in range(2) for j in range(2)]
    cross = [(j * 2 + k, k * 2 + 1 - j) for k in range(2) for j in range(2)]
    first = lax.ppermute(jnp.where(core_at == 0, done[0], done[1]), ("core", "zh"), same)
    second = lax.ppermute(jnp.where(core_at == 0, done[1], done[0]), ("core", "zh"), cross)
    halves = jnp.where(zh_at == 0, jnp.stack([first, second]), jnp.stack([second, first]))
    return halves.reshape(2, 160, 4, 160).transpose(0, 3, 2, 1).reshape(1, 1, 320, 640)


def solution(mesh):
    torus = Mesh(mesh.devices.reshape(4, 4, 2, 4, 2), ("x", "zl", "core", "y", "zh"))
    return jax.shard_map(
        on_device,
        mesh=torus,
        in_specs=(
            P(DP, HEAD, None, None),
            P(),
            P(),
            P(DP, None, HEAD),
            P(None, HEAD),
            P(HEAD + DP, None),
            P(HEAD),
            P(),
            P(),
            P(DP, HEAD),
            P(HEAD),
            P(HEAD + DP, None),
            P(HEAD),
            P(),
        ),
        out_specs=P(DP, HEAD, None, None),
        check_vma=False,
    )
```

profile of v0, /device:TPU:3, one launch (start us, length us, event | category | flops | bytes accessed | tf_op | source)
XLA Modules:
  0.0 857.3 jit_solution(10657175189306649570)
XLA Ops:
  13.1 9.3 %all-to-all-start = ((bf16[32,10,640]{2,1,0:T(8,128)(2,1)}), bf16[32,10,640]{2,1,0:T(8,128)(2,1)S(1)}, u32[]{:S(2)}, u32[]{:S(2)}) async-start(bf16[32,10,640]{2,1,0:T(8,128)(2,1)} %reshape.133), calls=%async_computation | async-start | bytes 1310720 | tf_op jit(solution)/shard_map/all_to_all | solution.py:14
  23.1 17.5 %all-to-all-done = bf16[32,10,640]{2,1,0:T(8,128)(2,1)S(1)} async-done(((bf16[32,10,640]{2,1,0:T(8,128)(2,1)}), bf16[32,10,640]{2,1,0:T(8,128)(2,1)S(1)}, u32[]{:S(2)}, u32[]{:S(2)}) %all-to-all-start) | async-done | bytes 409632 | tf_op jit(solution)/shard_map/all_to_all | solution.py:14
  41.4 28.5 %all_to_all.25 = bf16[32,10,640]{2,1,0:T(8,128)(2,1)S(1)} all-to-all(bf16[32,10,640]{2,1,0:T(8,128)(2,1)S(1)} %broadcast_select_fusion), channel_id=1, replica_groups=mesh['x'=4,'zl'=4,'core'=2,'y'=4,'zh'=2] {'zh','x','zl'}, dimensions={0} | all-to-all | bytes 819200 | tf_op jit(solution)/shard_map/all_to_all | solution.py:14
  71.4 4.6 all-to-all-start.2
  77.6 5.0 collective-permute-done
  82.6 13.7 %all-to-all-done.2 = bf16[4,320,640]{2,1,0:T(8,128)(2,1)S(1)} async-done(((bf16[4,320,640]{2,1,0:T(8,128)(2,1)}), bf16[4,320,640]{2,1,0:T(8,128)(2,1)S(1)}, u32[]{:S(2)}, u32[]{:S(2)}) %all-to-all-start.2) | async-done | bytes 1638432 | tf_op jit(solution)/shard_map/all_to_all | solution.py:14
  97.8 30.2 %all-gather.7.cloned.1.call-done = bf16[2560,384]{1,0:T(8,128)(2,1)} async-done(((bf16[40,384]{1,0:T(8,128)(2,1)}), bf16[2560,384]{1,0:T(8,128)(2,1)}) %all-gather.7.cloned.1.call-update) | async-done | bytes 1966096 | tf_op jit(solution)/shard_map/all_gather | solution.py:81
  145.1 4.3 all-to-all-start.3
  154.7 9.1 %collective-permute-done.1 = f32[320]{0:T(512)S(1)} collective-permute-done((f32[320]{0:T(512)S(1)}, f32[320]{0:T(512)S(1)}, u32[]{:S(2)}, u32[]{:S(2)}) %collective-permute-start.1) | collective-permute-done | bytes 1312 | tf_op jit(solution)/shard_map/ppermute | solution.py:96
  163.8 3.4 collective-permute-done.2
  170.1 373.0 %all-gather.11.cloned.1.call-done = bf16[256,4,1280]{2,1,0:T(4,128)(2,1)} async-done(((bf16[1,4,1280]{2,1,0:T(4,128)(2,1)}), bf16[256,4,1280]{2,1,0:T(4,128)(2,1)}) %all-gather.11.cloned.1.call-update) | async-done | bytes 2621456 | tf_op jit(solution)/shard_map/all_gather | solution.py:82
  543.1 5.3 reshape.150
  548.5 4.2 convert_reduce_fusion
  554.5 107.6 %all-gather.9.cloned.1.call-done = bf16[2560,640]{1,0:T(8,128)(2,1)} async-done(((bf16[40,640]{1,0:T(8,128)(2,1)}), bf16[2560,640]{1,0:T(8,128)(2,1)}) %all-gather.9.cloned.1.call-update) | async-done | bytes 3276816 | tf_op jit(solution)/shard_map/all_gather | solution.py:83
  662.2 5.0 fusion.61
  670.1 108.1 %all-gather.13.cloned.1.call-done = bf16[64,20,1280]{2,1,0:T(8,128)(2,1)} async-done(((bf16[1,20,1280]{2,1,0:T(8,128)(2,1)}), bf16[64,20,1280]{2,1,0:T(8,128)(2,1)}) %all-gather.13.cloned.1.call-update) | async-done | bytes 3276816 | tf_op jit(solution)/shard_map/all_gather | solution.py:84
  778.2 4.9 reshape.152
  783.1 12.1 %fusion.20 = bf16[1280,640]{0,1:T(8,128)(2,1)} fusion(bf16[1280,1280]{1,0:T(8,128)(2,1)S(1)} %reshape.152, f32[640,640]{1,0:T(8,128)} %fusion.64, f32[640,640]{1,0:T(8,128)} %fusion.61, f32[1280]{0:T(1024)S(1)} %add.183), kind=kOutput, calls=%fused_computation.47 | convolution fusion | flops 2152857600 | bytes 8197120 | tf_op jit(solution)/shard_map/dot_general | solution.py:32
  795.2 3.5 copy.38
  798.7 4.0 all-to-all-start.4
  802.8 20.9 %all-to-all-done.4 = bf16[4,320,640]{2,1,0:T(8,128)(2,1)S(1)} async-done(((bf16[4,320,640]{2,1,0:T(8,128)(2,1)}), bf16[4,320,640]{2,1,0:T(8,128)(2,1)S(1)}, u32[]{:S(2)}, u32[]{:S(2)}) %all-to-all-start.4) | async-done | bytes 1638432 | tf_op jit(solution)/shard_map/all_to_all | solution.py:14
  825.7 6.3 collective-permute-start.5
  832.1 13.2 %collective-permute-done.5 = bf16[160,640]{0,1:T(8,128)(2,1)S(1)} collective-permute-done((bf16[160,640]{0,1:T(8,128)(2,1)S(1)}, bf16[160,640]{0,1:T(8,128)(2,1)S(1)}, u32[]{:S(2)}, u32[]{:S(2)}) %collective-permute-start.5) | collective-permute-done | bytes 204832 | tf_op jit(solution)/shard_map/ppermute | solution.py:133
  845.3 3.3 collective-permute-done.6
  (128 shorter events, 46.4 us)
Async XLA Ops:
  6.5 15.9 %copy-start.15 = (s32[32]{0:T(128)S(1)}, s32[32]{0:T(128)}, u32[]{:S(2)}) copy-start(s32[32]{0:T(128)} %param.27) | copy-start | bytes 388
  6.5 121.4 %all-gather.7.cloned.1.call-start = ((), (), s32[]{:S(2)}) async-start(), calls=%async_computation.5 | async-start | bytes 1996800 | tf_op jit(solution)/shard_map/all_gather | solution.py:81
  7.9 535.2 %all-gather.11.cloned.1.call-start = ((), (), s32[]{:S(2)}) async-start(), calls=%async_computation.7 | async-start | bytes 2631680 | tf_op jit(solution)/shard_map/all_gather | solution.py:82
  8.7 653.5 %all-gather.9.cloned.1.call-start = ((), (), s32[]{:S(2)}) async-start(), calls=%async_computation.6 | async-start | bytes 3328000 | tf_op jit(solution)/shard_map/all_gather | solution.py:83
  13.1 27.5 %all-to-all-start = ((bf16[32,10,640]{2,1,0:T(8,128)(2,1)}), bf16[32,10,640]{2,1,0:T(8,128)(2,1)S(1)}, u32[]{:S(2)}, u32[]{:S(2)}) async-start(bf16[32,10,640]{2,1,0:T(8,128)(2,1)} %reshape.133), calls=%async_computation | async-start | bytes 1310720 | tf_op jit(solution)/shard_map/all_to_all | solution.py:14
  69.9 6.1 copy-start.10
  71.4 25.7 %copy-start.5 = (f32[1280]{0:T(1024)S(1)}, f32[1280]{0:T(1024)}, u32[]{:S(2)}) copy-start(f32[1280]{0:T(1024)} %param.16) | copy-start | bytes 15364
  71.4 25.7 %copy-start.6 = (f32[1280]{0:T(1024)S(1)}, f32[1280]{0:T(1024)}, u32[]{:S(2)}) copy-start(f32[1280]{0:T(1024)} %param.15) | copy-start | bytes 15364
  71.4 24.9 %all-to-all-start.2 = ((bf16[4,320,640]{2,1,0:T(8,128)(2,1)}), bf16[4,320,640]{2,1,0:T(8,128)(2,1)S(1)}, u32[]{:S(2)}, u32[]{:S(2)}) async-start(bf16[4,320,640]{2,1,0:T(8,128)(2,1)} %broadcast_in_dim.38), calls=%async_computation.2 | async-start | bytes 3276800 | tf_op jit(solution)/shard_map/all_to_all | solution.py:14
  76.0 702.2 %all-gather.13.cloned.1.call-start = ((), (), s32[]{:S(2)}) async-start(), calls=%async_computation.8 | async-start | bytes 3993600 | tf_op jit(solution)/shard_map/all_gather | solution.py:84
  76.2 6.4 collective-permute-start
  132.4 2.9 collective-permute-start.4
  145.1 403.4 %all-to-all-start.3 = ((bf16[4,256,640]{2,1,0:T(8,128)(2,1)}), bf16[4,256,640]{2,1,0:T(8,128)(2,1)}, u32[]{:S(2)}, u32[]{:S(2)}) async-start(bf16[4,256,640]{2,1,0:T(8,128)(2,1)} %broadcast_in_dim.43), calls=%async_computation.3 | async-start | bytes 2621440 | tf_op jit(solution)/shard_map/all_to_all | solution.py:14
  149.6 14.2 %collective-permute-start.1 = (f32[320]{0:T(512)S(1)}, f32[320]{0:T(512)S(1)}, u32[]{:S(2)}, u32[]{:S(2)}) collective-permute-start(f32[320]{0:T(512)S(1)} %reshape.135), channel_id=1, source_target_pairs={{0,2},{2,4},{4,6},{6,0},{1,3},{3,5},{5,7},{7,1},{8,10},{10,12},{12... | collective-permute-start | bytes 3848 | tf_op jit(solution)/shard_map/ppermute | solution.py:96
  151.0 16.2 %collective-permute-start.2 = (f32[320]{0:T(512)S(1)}, f32[320]{0:T(512)S(1)}, u32[]{:S(2)}, u32[]{:S(2)}) collective-permute-start(f32[320]{0:T(512)S(1)} %reshape.135), channel_id=1, source_target_pairs={{0,4},{2,6},{4,0},{6,2},{1,5},{3,7},{5,1},{7,3},{8,12},{10,14},{12... | collective-permute-start | bytes 3848 | tf_op jit(solution)/shard_map/ppermute | solution.py:96
  153.3 13.9 %collective-permute-start.3 = (f32[320]{0:T(512)S(1)}, f32[320]{0:T(512)S(1)}, u32[]{:S(2)}, u32[]{:S(2)}) collective-permute-start(f32[320]{0:T(512)S(1)} %reshape.135), channel_id=1, source_target_pairs={{0,6},{2,0},{4,2},{6,4},{1,7},{3,1},{5,3},{7,5},{8,14},{10,8},{12,... | collective-permute-start | bytes 3848 | tf_op jit(solution)/shard_map/ppermute | solution.py:96
  170.1 378.3 %copy-start.2 = (f32[1280,640]{0,1:T(8,128)S(1)}, f32[1280,640]{0,1:T(8,128)}, u32[]{:S(2)}) copy-start(f32[1280,640]{0,1:T(8,128)} %copy.36) | copy-start | bytes 9830404
  548.4 113.8 %copy-start.13 = (f32[1280]{0:T(1024)S(1)}, f32[1280]{0:T(1024)}, u32[]{:S(2)}) copy-start(f32[1280]{0:T(1024)} %param.22) | copy-start | bytes 15364
  548.4 113.8 %copy-start.14 = (f32[1280]{0:T(1024)S(1)}, f32[1280]{0:T(1024)}, u32[]{:S(2)}) copy-start(f32[1280]{0:T(1024)} %param.21) | copy-start | bytes 15364
  554.5 112.6 %copy-start.4 = (bf16[1280,640]{0,1:T(8,128)(2,1)S(1)}, bf16[1280,640]{0,1:T(8,128)(2,1)}, u32[]{:S(2)}) copy-start(bf16[1280,640]{0,1:T(8,128)(2,1)} %copy-done.3) | copy-start | bytes 4915204
  798.7 24.9 %all-to-all-start.4 = ((bf16[4,320,640]{2,1,0:T(8,128)(2,1)}), bf16[4,320,640]{2,1,0:T(8,128)(2,1)S(1)}, u32[]{:S(2)}, u32[]{:S(2)}) async-start(bf16[4,320,640]{2,1,0:T(8,128)(2,1)} %bitcast.17), calls=%async_computation.4 | async-start | bytes 3276800 | tf_op jit(solution)/shard_map/all_to_all | solution.py:14
  823.9 26.7 %copy-start.1 = (bf16[40,3,128]{2,0,1:T(8,128)(2,1)S(1)}, bf16[40,3,128]{2,0,1:T(8,128)(2,1)}, u32[]{:S(2)}) copy-start(bf16[40,3,128]{2,0,1:T(8,128)(2,1)} %param.17) | copy-start | bytes 92164
  825.7 19.6 %collective-permute-start.5 = (bf16[160,640]{0,1:T(8,128)(2,1)S(1)}, bf16[160,640]{0,1:T(8,128)(2,1)S(1)}, u32[]{:S(2)}, u32[]{:S(2)}) collective-permute-start(bf16[160,640]{0,1:T(8,128)(2,1)S(1)} %get-tuple-element.11), channel_id=1, source_target_pairs={{0,0},{8,1},{1,8},{9,9},{2,2},{10,3},{3,10},{11,11},{4,4},{12,5},{... | collective-permute-start | bytes 614408 | tf_op jit(solution)/shard_map/ppermute | solution.py:133
  832.0 16.6 %collective-permute-start.6 = (bf16[160,640]{0,1:T(8,128)(2,1)S(1)}, bf16[160,640]{0,1:T(8,128)(2,1)S(1)}, u32[]{:S(2)}, u32[]{:S(2)}) collective-permute-start(bf16[160,640]{0,1:T(8,128)(2,1)S(1)} %get-tuple-element.12), channel_id=1, source_target_pairs={{0,1},{8,0},{1,9},{9,8},{2,3},{10,2},{3,11},{11,10},{4,5},{12,4},{... | collective-permute-start | bytes 614408 | tf_op jit(solution)/shard_map/ppermute | solution.py:134
  (7 other events, 27.7 us)
Sparse Core Ops, SparseCore 0:
  9.2 118.7 all-gather.6
  129.8 413.2 all-gather.10
  545.0 117.1 all-gather.8
  663.9 114.2 all-gather.12
where the time goes:
time: 864 us; the launch traced here: 857 us
  waiting for transfers between devices  708 us (82%)
  starting transfers between devices  35.8 us (4%)
  matrix products  32.8 us (4%)
  local copies, waits for them, and re-layouts  29.2 us (3%)
  blocking collectives  28.5 us (3%)
  between operations  13.8 us (2%)
  other arithmetic  8.8 us (1%)
    all_gather x1, waiting for transfers between devices, on_device(): w_out = lax.all_gather(out_weight, ('y',) + plane, axis=0, tiled=True)  373 us
    all_gather x1, waiting for transfers between devices, on_device(): w_two = lax.all_gather(fc2_weight, plane, axis=0, tiled=True)  108 us
    all_gather x1, waiting for transfers between devices, on_device(): w_one = lax.all_gather(fc1_weight, plane, axis=0, tiled=True)  108 us
    all_to_all x4, waiting for transfers between devices, exchange(): return lax.all_to_all(value, axes, split_axis=0, concat_axis=0, tiled=True)  52 us
    all_gather x1, waiting for transfers between devices, on_device(): lax.all_gather(qkv_weight.reshape(40, 384), plane, axis=0, tiled=True)  30.2 us
    dot_general x10, matrix products, dot_rows(): lax.dot_general(left, right, (((0,), (0,)), ((), ())), preferred_element_...  30.1 us
    all_to_all x1, blocking collectives, exchange(): return lax.all_to_all(value, axes, split_axis=0, concat_axis=0, tiled=True)  28.5 us
    all_to_all x4, starting transfers between devices, exchange(): return lax.all_to_all(value, axes, split_axis=0, concat_axis=0, tiled=True)  22.3 us
  transfers between devices with their start and end apart: 15, of which 13 were waited for; matrix products, arithmetic and copies ran while one was open for 5% of the time, Pallas kernels for 0%

commit v1 on v0

--- a/solution.py
+++ b/solution.py
@@ -81,7 +81,9 @@
     w_qkv = lax.all_gather(qkv_weight.reshape(40, 384), plane, axis=0, tiled=True)
     w_out = lax.all_gather(out_weight, ("y",) + plane, axis=0, tiled=True)
     w_one = lax.all_gather(fc1_weight, plane, axis=0, tiled=True)
-    w_two = lax.all_gather(fc2_weight, plane, axis=0, tiled=True)
+    w_two = jnp.concatenate(
+        lax.all_to_all(jnp.stack([fc2_weight] * lax.axis_size(plane)), plane, 0, 0), axis=0
+    )
     own = jnp.concatenate([qv_bias[0], qv_bias[1], fc1_bias, fc2_bias, out_bias])
     other = lax.ppermute(own, "zh", [(0, 1), (1, 0)])
     both = jnp.where(zh_at == 0, jnp.stack([own, other]), jnp.stack([other, own]))

time: 864 us -> 780 us (0.903)
  waiting for transfers between devices: 708 us -> 613 us
    all_gather x1 -> x0, waiting for transfers between devices: 108 us -> none  [on_device(): w_two = lax.all_gather(fc2_weight, plane, axis=0, tiled=True)]
    all_gather x1, waiting for transfers between devices: 30.2 us -> 48.2 us  [on_device(): lax.all_gather(qkv_weight.reshape(40, 384), plane, axis=0, tiled=True)]
    all_to_all x4, waiting for transfers between devices: 52 us -> 64.9 us  [exchange(): return lax.all_to_all(value, axes, split_axis=0, concat_axis=0, tiled=True)]
    ppermute x3, waiting for transfers between devices: 12.5 us -> 1.83 us  [on_device(): lax.ppermute(out_pair, 'y', [(at, (at + step) % 4) for at in range(4)])]
    all_to_all x0 -> x1, starting transfers between devices: none -> 9.47 us  [on_device(): lax.all_to_all(jnp.stack([fc2_weight] * lax.axis_size(plane)), plane, 0, 0)]
  transfers between devices with their start and end apart: 15 -> 15, of which waited for: 13 -> 14; matrix products, arithmetic and copies ran while one was open for 5% -> 5% of each run, Pallas kernels for 0% -> 0%
where the time goes in v1:
time: 780 us; the launch traced here: 770 us
  waiting for transfers between devices  613 us (79%)
  starting transfers between devices  44.1 us (6%)
  matrix products  32.8 us (4%)
  local copies, waits for them, and re-layouts  29.4 us (4%)
  blocking collectives  26.5 us (3%)
  between operations  15.5 us (2%)
  other arithmetic  8.81 us (1%)
    all_gather x1, waiting for transfers between devices, on_device(): w_out = lax.all_gather(out_weight, ('y',) + plane, axis=0, tiled=True)  374 us
    all_gather x1, waiting for transfers between devices, on_device(): w_one = lax.all_gather(fc1_weight, plane, axis=0, tiled=True)  105 us
    all_to_all x4, waiting for transfers between devices, exchange(): return lax.all_to_all(value, axes, split_axis=0, concat_axis=0, tiled=True)  64.9 us
    all_gather x1, waiting for transfers between devices, on_device(): lax.all_gather(qkv_weight.reshape(40, 384), plane, axis=0, tiled=True)  48.2 us
    dot_general x10, matrix products, dot_rows(): lax.dot_general(left, right, (((0,), (0,)), ((), ())), preferred_element_...  30 us
    all_to_all x1, blocking collectives, exchange(): return lax.all_to_all(value, axes, split_axis=0, concat_axis=0, tiled=True)  26.5 us
    all_to_all x4, starting transfers between devices, exchange(): return lax.all_to_all(value, axes, split_axis=0, concat_axis=0, tiled=True)  21.9 us
  transfers between devices with their start and end apart: 15, of which 14 were waited for; matrix products, arithmetic and copies ran while one was open for 5% of the time, Pallas kernels for 0%

profile of v1, /device:TPU:3, one launch (start us, length us, event | category | flops | bytes accessed | tf_op | source)
XLA Modules:
  0.0 770.4 jit_solution(454032891740214003)
XLA Ops:
  11.0 9.3 %all-to-all-start = ((bf16[32,10,640]{2,1,0:T(8,128)(2,1)}), bf16[32,10,640]{2,1,0:T(8,128)(2,1)S(1)}, u32[]{:S(2)}, u32[]{:S(2)}) async-start(bf16[32,10,640]{2,1,0:T(8,128)(2,1)} %reshape.138), calls=%async_computation | async-start | bytes 1310720 | tf_op jit(solution)/shard_map/all_to_all | solution.py:14
  21.8 15.7 %all-to-all-done = bf16[32,10,640]{2,1,0:T(8,128)(2,1)S(1)} async-done(((bf16[32,10,640]{2,1,0:T(8,128)(2,1)}), bf16[32,10,640]{2,1,0:T(8,128)(2,1)S(1)}, u32[]{:S(2)}, u32[]{:S(2)}) %all-to-all-start) | async-done | bytes 409632 | tf_op jit(solution)/shard_map/all_to_all | solution.py:14
  38.4 26.5 %all_to_all.30 = bf16[32,10,640]{2,1,0:T(8,128)(2,1)S(1)} all-to-all(bf16[32,10,640]{2,1,0:T(8,128)(2,1)S(1)} %broadcast_select_fusion), channel_id=1, replica_groups=mesh['x'=4,'zl'=4,'core'=2,'y'=4,'zh'=2] {'zh','x','zl'}, dimensions={0} | all-to-all | bytes 819200 | tf_op jit(solution)/shard_map/all_to_all | solution.py:14
  66.4 4.6 all-to-all-start.2
  73.4 4.1 collective-permute-done
  77.5 11.5 %all-to-all-done.2 = bf16[4,320,640]{2,1,0:T(8,128)(2,1)S(1)} async-done(((bf16[4,320,640]{2,1,0:T(8,128)(2,1)}), bf16[4,320,640]{2,1,0:T(8,128)(2,1)S(1)}, u32[]{:S(2)}, u32[]{:S(2)}) %all-to-all-start.2) | async-done | bytes 1638432 | tf_op jit(solution)/shard_map/all_to_all | solution.py:14
  90.5 48.2 %all-gather.5.cloned.1.call-done = bf16[2560,384]{1,0:T(8,128)(2,1)} async-done(((bf16[40,384]{1,0:T(8,128)(2,1)}), bf16[2560,384]{1,0:T(8,128)(2,1)}) %all-gather.5.cloned.1.call-update) | async-done | bytes 1966096 | tf_op jit(solution)/shard_map/all_gather | solution.py:81
  155.8 4.0 all-to-all-start.3
  160.4 16.9 %all-to-all-done.3 = bf16[4,256,640]{2,1,0:T(8,128)(2,1)S(1)} async-done(((bf16[4,256,640]{2,1,0:T(8,128)(2,1)}), bf16[4,256,640]{2,1,0:T(8,128)(2,1)S(1)}, u32[]{:S(2)}, u32[]{:S(2)}) %all-to-all-start.3) | async-done | bytes 1310752 | tf_op jit(solution)/shard_map/all_to_all | solution.py:14
  179.4 9.5 %all-to-all-start.4 = ((bf16[64,20,1280]{2,1,0:T(8,128)(2,1)}), bf16[64,20,1280]{2,1,0:T(8,128)(2,1)}, u32[]{:S(2)}, u32[]{:S(2)}) async-start(bf16[64,20,1280]{2,1,0:T(8,128)(2,1)} %stack.22), calls=%async_computation.4 | async-start | bytes 7864320 | tf_op jit(solution)/shard_map/all_to_all | solution.py:85
  194.2 2.5 copy.36
  196.7 374.4 %all-gather.9.cloned.1.call-done = bf16[256,4,1280]{2,1,0:T(4,128)(2,1)} async-done(((bf16[1,4,1280]{2,1,0:T(4,128)(2,1)}), bf16[256,4,1280]{2,1,0:T(4,128)(2,1)}) %all-gather.9.cloned.1.call-update) | async-done | bytes 2621456 | tf_op jit(solution)/shard_map/all_gather | solution.py:82
  571.1 5.3 reshape.156
  576.4 4.8 convert_reduce_fusion
  581.9 104.6 %all-gather.7.cloned.1.call-done = bf16[2560,640]{1,0:T(8,128)(2,1)} async-done(((bf16[40,640]{1,0:T(8,128)(2,1)}), bf16[2560,640]{1,0:T(8,128)(2,1)}) %all-gather.7.cloned.1.call-update) | async-done | bytes 3276816 | tf_op jit(solution)/shard_map/all_gather | solution.py:83
  686.4 4.5 fusion.61
  690.9 3.0 fusion.64
  693.9 6.3 reshape.143
  700.3 11.9 %fusion.20 = bf16[1280,640]{0,1:T(8,128)(2,1)S(1)} fusion(bf16[1280,1280]{1,0:T(8,128)(2,1)} %reshape.143, f32[640,640]{1,0:T(8,128)} %fusion.64, f32[640,640]{1,0:T(8,128)} %fusion.61, f32[1280]{0:T(1024)S(1)} %add.183), kind=kOutput, calls=%fused_computation.47 | convolution fusion | flops 2152857600 | bytes 8197120 | tf_op jit(solution)/shard_map/dot_general | solution.py:32
  714.4 4.0 all-to-all-start.5
  718.5 20.9 %all-to-all-done.5 = bf16[4,320,640]{2,1,0:T(8,128)(2,1)S(1)} async-done(((bf16[4,320,640]{2,1,0:T(8,128)(2,1)}), bf16[4,320,640]{2,1,0:T(8,128)(2,1)S(1)}, u32[]{:S(2)}, u32[]{:S(2)}) %all-to-all-start.5) | async-done | bytes 1638432 | tf_op jit(solution)/shard_map/all_to_all | solution.py:14
  741.4 6.6 collective-permute-start.5
  748.1 8.3 %collective-permute-done.5 = bf16[160,640]{0,1:T(8,128)(2,1)S(1)} collective-permute-done((bf16[160,640]{0,1:T(8,128)(2,1)S(1)}, bf16[160,640]{0,1:T(8,128)(2,1)S(1)}, u32[]{:S(2)}, u32[]{:S(2)}) %collective-permute-start.5) | collective-permute-done | bytes 204832 | tf_op jit(solution)/shard_map/ppermute | solution.py:135
  756.5 4.4 collective-permute-done.6
  (126 shorter events, 43.1 us)
Async XLA Ops:
  7.4 13.1 %copy-start = (bf16[40,3,128]{2,0,1:T(8,128)(2,1)S(1)}, bf16[40,3,128]{2,0,1:T(8,128)(2,1)}, u32[]{:S(2)}) copy-start(bf16[40,3,128]{2,0,1:T(8,128)(2,1)} %param.17) | copy-start | bytes 92164
  7.4 13.8 %copy-start.14 = (s32[32]{0:T(128)S(1)}, s32[32]{0:T(128)}, u32[]{:S(2)}) copy-start(s32[32]{0:T(128)} %param.27) | copy-start | bytes 388
  11.0 26.5 %all-to-all-start = ((bf16[32,10,640]{2,1,0:T(8,128)(2,1)}), bf16[32,10,640]{2,1,0:T(8,128)(2,1)S(1)}, u32[]{:S(2)}, u32[]{:S(2)}) async-start(bf16[32,10,640]{2,1,0:T(8,128)(2,1)} %reshape.138), calls=%async_computation | async-start | bytes 1310720 | tf_op jit(solution)/shard_map/all_to_all | solution.py:14
  20.4 118.2 %all-gather.5.cloned.1.call-start = ((), (), s32[]{:S(2)}) async-start(), calls=%async_computation.6 | async-start | bytes 1996800 | tf_op jit(solution)/shard_map/all_gather | solution.py:81
  66.4 23.5 %copy-start.4 = (f32[1280]{0:T(1024)S(1)}, f32[1280]{0:T(1024)}, u32[]{:S(2)}) copy-start(f32[1280]{0:T(1024)} %param.16) | copy-start | bytes 15364
  66.4 23.5 %copy-start.5 = (f32[1280]{0:T(1024)S(1)}, f32[1280]{0:T(1024)}, u32[]{:S(2)}) copy-start(f32[1280]{0:T(1024)} %param.15) | copy-start | bytes 15364
  66.4 22.6 %all-to-all-start.2 = ((bf16[4,320,640]{2,1,0:T(8,128)(2,1)}), bf16[4,320,640]{2,1,0:T(8,128)(2,1)S(1)}, u32[]{:S(2)}, u32[]{:S(2)}) async-start(bf16[4,320,640]{2,1,0:T(8,128)(2,1)} %broadcast_in_dim.38), calls=%async_computation.2 | async-start | bytes 3276800 | tf_op jit(solution)/shard_map/all_to_all | solution.py:14
  70.9 500.2 %all-gather.9.cloned.1.call-start = ((), (), s32[]{:S(2)}) async-start(), calls=%async_computation.8 | async-start | bytes 2631680 | tf_op jit(solution)/shard_map/all_gather | solution.py:82
  71.0 6.4 collective-permute-start
  143.1 2.9 collective-permute-start.4
  154.6 22.7 %copy-start.3 = (bf16[20,1280]{1,0:T(8,128)(2,1)S(1)}, bf16[20,1280]{1,0:T(8,128)(2,1)}, u32[]{:S(2)}) copy-start(bf16[20,1280]{1,0:T(8,128)(2,1)} %param.25) | copy-start | bytes 153604
  155.8 21.5 %all-to-all-start.3 = ((bf16[4,256,640]{2,1,0:T(8,128)(2,1)}), bf16[4,256,640]{2,1,0:T(8,128)(2,1)S(1)}, u32[]{:S(2)}, u32[]{:S(2)}) async-start(bf16[4,256,640]{2,1,0:T(8,128)(2,1)} %broadcast_in_dim.43), calls=%async_computation.3 | async-start | bytes 2621440 | tf_op jit(solution)/shard_map/all_to_all | solution.py:14
  159.8 526.6 %all-gather.7.cloned.1.call-start = ((), (), s32[]{:S(2)}) async-start(), calls=%async_computation.7 | async-start | bytes 3328000 | tf_op jit(solution)/shard_map/all_gather | solution.py:83
  179.4 514.5 %all-to-all-start.4 = ((bf16[64,20,1280]{2,1,0:T(8,128)(2,1)}), bf16[64,20,1280]{2,1,0:T(8,128)(2,1)}, u32[]{:S(2)}, u32[]{:S(2)}) async-start(bf16[64,20,1280]{2,1,0:T(8,128)(2,1)} %stack.22), calls=%async_computation.4 | async-start | bytes 7864320 | tf_op jit(solution)/shard_map/all_to_all | solution.py:85
  189.1 3.9 collective-permute-start.1
  189.4 4.3 collective-permute-start.2
  191.1 2.8 collective-permute-start.3
  576.4 110.0 %copy-start.12 = (f32[1280]{0:T(1024)S(1)}, f32[1280]{0:T(1024)}, u32[]{:S(2)}) copy-start(f32[1280]{0:T(1024)} %param.22) | copy-start | bytes 15364
  576.4 110.0 %copy-start.13 = (f32[1280]{0:T(1024)S(1)}, f32[1280]{0:T(1024)}, u32[]{:S(2)}) copy-start(f32[1280]{0:T(1024)} %param.21) | copy-start | bytes 15364
  581.3 109.7 %copy-start.2 = (bf16[1280,640]{0,1:T(8,128)(2,1)}, bf16[1280,640]{0,1:T(8,128)(2,1)S(1)}, u32[]{:S(2)}) copy-start(bf16[1280,640]{0,1:T(8,128)(2,1)S(1)} %get-tuple-element.6) | copy-start | bytes 4915204
  714.4 24.9 %all-to-all-start.5 = ((bf16[4,320,640]{2,1,0:T(8,128)(2,1)}), bf16[4,320,640]{2,1,0:T(8,128)(2,1)S(1)}, u32[]{:S(2)}, u32[]{:S(2)}) async-start(bf16[4,320,640]{2,1,0:T(8,128)(2,1)} %bitcast.16), calls=%async_computation.5 | async-start | bytes 3276800 | tf_op jit(solution)/shard_map/all_to_all | solution.py:14
  739.5 23.2 %copy-start.1 = (bf16[40,3,128]{2,0,1:T(8,128)(2,1)S(1)}, bf16[40,3,128]{2,0,1:T(8,128)(2,1)}, u32[]{:S(2)}) copy-start(bf16[40,3,128]{2,0,1:T(8,128)(2,1)} %param.17) | copy-start | bytes 92164
  741.4 15.1 %collective-permute-start.5 = (bf16[160,640]{0,1:T(8,128)(2,1)S(1)}, bf16[160,640]{0,1:T(8,128)(2,1)S(1)}, u32[]{:S(2)}, u32[]{:S(2)}) collective-permute-start(bf16[160,640]{0,1:T(8,128)(2,1)S(1)} %get-tuple-element.11), channel_id=1, source_target_pairs={{0,0},{8,1},{1,8},{9,9},{2,2},{10,3},{3,10},{11,11},{4,4},{12,5},{... | collective-permute-start | bytes 614408 | tf_op jit(solution)/shard_map/ppermute | solution.py:135
  748.0 12.9 %collective-permute-start.6 = (bf16[160,640]{0,1:T(8,128)(2,1)S(1)}, bf16[160,640]{0,1:T(8,128)(2,1)S(1)}, u32[]{:S(2)}, u32[]{:S(2)}) collective-permute-start(bf16[160,640]{0,1:T(8,128)(2,1)S(1)} %get-tuple-element.12), channel_id=1, source_target_pairs={{0,1},{8,0},{1,9},{9,8},{2,3},{10,2},{3,11},{11,10},{4,5},{12,4},{... | collective-permute-start | bytes 614408 | tf_op jit(solution)/shard_map/ppermute | solution.py:136
  (6 other events, 31.0 us)
Sparse Core Ops, SparseCore 0:
  23.1 115.5 all-gather.4
Sparse Core Ops, SparseCore 1:
  144.0 427.1 all-gather.8
  572.9 113.5 all-gather.6
